TPU v7x, 32 devices: a whole 2x2x4 slice. The times are simulated.
32 devices in a mesh: members: 2 (over y), stars: 16 (over z, x, core).
Axes of the slice: x: 2, y: 2, z: 4, core: 2. Of those that a mesh axis runs over, the one named last changes fastest.
Arguments:
- position: float32 [3, 8192], P(None, ('members', 'stars')), parts along dimension 1, may hold values from -8 to 8
- velocity: float32 [3, 8192], P(None, ('members', 'stars')), parts along dimension 1, may hold values from -2 to 2
- acceleration: float32 [3, 8192], P(None, ('members', 'stars')), parts along dimension 1, may hold values from -2 to 2
- old_jerk: float32 [3, 8192], P(None, ('members', 'stars')), parts along dimension 1, may hold values from -6 to 6
- masses: float32 [8192], P(('members', 'stars')), parts along dimension 0, may hold values from 4.8828126e-05 to 0.0012207031
- levels: int32 [8192], P(('members', 'stars')), parts along dimension 0, may hold values from 0 to 3
- active_count: int32 [32], P(('members', 'stars')), parts along dimension 0, may hold values from 0 to 32, as said below
- active_slot: int32 [1024], P(('members', 'stars')), parts along dimension 0, may hold values from 0 to 255, as said below
Outputs:
- corrected: float32 [4, 3, 1024], P(None, None, ('members', 'stars')), parts along dimension 2
- derivatives: float32 [2, 3, 1024], P(None, None, ('members', 'stars')), parts along dimension 2
There are 2 independent parts, one for each index of `members`. A program takes and returns all parts, laid end to end along the dimension named above; each array names one. Nothing has to cross between parts.
Inputs may be any that keep to these rules, and one draw needn't show every extreme that they name: `active_count`: the entries sum to 256; some entry equals 32 and some equals 0. `active_slot`: the 32 entries of one group are distinct; only its first active_count entries are live.
All inputs are finite; a program needn't handle non-finite values.
Results may differ from a plain program's by a relative error of at most 0.00002.
Values sent between devices are 32-bit elements; how exact they have to be, the bound alone decides.
No kernel may reach another device: no remote copies, remote signals or barrier semaphores. Data moves between devices by JAX's collectives and lax.ppermute only.
A program may use at most 64 MiB of HBM per device.

v0:
```python
import math

import jax
import jax.numpy as jnp
from jax import lax
from jax.sharding import PartitionSpec as P

SOFTEN = 0.0025
STEP_BASE = 0.5


def pair_terms(targets, res_pos, res_vel, res_mass):
    separation = res_pos[:, None, :] - targets[0:3, :, None]
    relative = res_vel[:, None, :] - targets[3:6, :, None]
    squared = jnp.sum(separation * separation, axis=0) + SOFTEN
    inverse = lax.rsqrt(squared)
    inverse_sq = inverse * inverse
    weight = res_mass[None, :] * inverse * inverse_sq
    radial = 3.0 * jnp.sum(separation * relative, axis=0) * inverse_sq
    pull = jnp.sum(weight[None] * separation, axis=2)
    jerk_sum = jnp.sum(weight[None] * (relative - radial[None] * separation), axis=2)
    return jnp.concatenate([pull, jerk_sum], axis=0)


def forces(targets, res_pos, res_vel, res_mass, block_limit):
    row_total = targets.shape[1]
    block_rows = row_total if row_total <= block_limit else math.gcd(row_total, block_limit)
    block_count = row_total // block_rows
    target_tiles = targets.reshape(6, block_count, block_rows).transpose(1, 0, 2)

    def one_tile(tile_cols):
        return pair_terms(tile_cols, res_pos, res_vel, res_mass)

    result = lax.map(one_tile, target_tiles)
    return result.transpose(1, 0, 2).reshape(6, row_total)


def shards(position, velocity, acceleration, old_jerk, masses, levels, active_count, active_slot):
    capacity = active_slot.shape[0]
    interval_all = STEP_BASE * jnp.exp2(-levels.astype(jnp.float32))
    moved_pos = position + interval_all * (
        velocity + interval_all * (0.5 * acceleration + interval_all * old_jerk / 6.0)
    )
    moved_vel = velocity + interval_all * (acceleration + 0.5 * interval_all * old_jerk)
    live = jnp.arange(capacity, dtype=jnp.int32) < active_count[0]
    targets = jnp.concatenate([moved_pos[:, active_slot], moved_vel[:, active_slot]], axis=0)
    targets = jnp.where(live[None, :], targets, 0.0)
    partial_value = forces(
        lax.all_gather(targets, "stars", axis=1, tiled=True), moved_pos, moved_vel, masses, 512
    )
    own_sums = lax.psum_scatter(partial_value, "stars", scatter_dimension=1, tiled=True)
    new_acc = own_sums[0:3]
    new_jerk = own_sums[3:6]
    interval = interval_all[active_slot]
    start_pos = position[:, active_slot]
    start_vel = velocity[:, active_slot]
    start_acc = acceleration[:, active_slot]
    start_jerk = old_jerk[:, active_slot]
    end_vel = (
        start_vel
        + 0.5 * interval * (start_acc + new_acc)
        + interval * interval * (start_jerk - new_jerk) / 12.0
    )
    end_pos = (
        start_pos
        + 0.5 * interval * (start_vel + end_vel)
        + interval * interval * (start_acc - new_acc) / 12.0
    )
    differ = start_acc - new_acc
    snap_term = 3.0 * differ + interval * (start_jerk + 2.0 * new_jerk)
    crackle_term = 2.0 * differ + interval * (start_jerk + new_jerk)
    corrected = jnp.where(live[None, None], jnp.stack([end_pos, end_vel, new_acc, new_jerk]), 0.0)
    derivatives = jnp.where(live[None, None], jnp.stack([snap_term, crackle_term]), 0.0)
    return (corrected, derivatives)


def solution(mesh):
    return jax.shard_map(
        shards,
        mesh=mesh,
        in_specs=(
            P(None, ("members", "stars")),
            P(None, ("members", "stars")),
            P(None, ("members", "stars")),
            P(None, ("members", "stars")),
            P(("members", "stars")),
            P(("members", "stars")),
            P(("members", "stars")),
            P(("members", "stars")),
        ),
        out_specs=(P(None, None, ("members", "stars")), P(None, None, ("members", "stars"))),
        check_vma=False,
    )
```

profile of v0, /device:TPU:0, one launch (start us, length us, event | category | flops | bytes accessed | tf_op | source)
XLA Modules:
  0.0 99.9 jit_solution(3401714419971519043)
XLA Ops:
  7.2 0.7 broadcast_multiply_fusion.1
  7.9 0.8 multiply_add_fusion.1
  8.7 0.1 copy.161
  8.8 0.7 compare_select_fusion
  9.5 0.6 gather_fusion.4
  10.0 0.1 copy.163
  10.1 0.1 copy.162
  10.3 0.6 gather_fusion.5
  10.8 0.1 copy.164
  11.6 23.3 %all-gather = f32[16,32,6]{1,2,0:T(8,128)S(1)} all-gather(f32[1,32,6]{1,2,0:T(8,128)S(1)} %fusion.5), channel_id=1, replica_groups=mesh['members'=2,'stars'=16] {'stars'}, dimensions={0}, use_global_device_ids=true | all-gather | bytes 13056 | tf_op jit(solution)/shard_map/all_gather | solution.py:49
  34.9 0.1 reshape.122
  35.0 0.5 fusion.2
  35.5 0.2 copy-done.4
  35.7 0.1 multiply_multiply_fusion
  35.8 0.9 fusion.3
  36.7 0.8 copy.170
  37.6 0.7 gather_fusion.1
  38.3 0.1 copy.155
  38.5 0.1 copy.157
  38.6 0.1 copy.159
  38.8 0.1 copy.166
  38.9 0.6 gather_fusion
  39.5 0.1 copy.156
  39.6 0.6 gather_fusion.2
  40.2 0.1 copy.158
  40.3 0.6 gather_fusion.3
  40.8 0.1 copy.160
  40.9 0.6 gather_fusion.6
  41.6 49.2 %reduce-scatter.4.cloned.1.call-done = f32[32,6]{1,0:T(8,128)} async-done(((f32[512,6]{1,0:T(8,128)}), f32[32,6]{1,0:T(8,128)}) %reduce-scatter.4.cloned.1.call-update) | async-done | bytes 784
  90.8 0.9 fusion.22
  91.9 0.6 copy.169
  92.4 0.6 copy.168
  (24 shorter events, 0.4 us)
Async XLA Ops:
  7.2 83.6 %reduce-scatter.4.cloned.1.call-start = ((), (), s32[]{:S(2)}) async-start(), calls=%async_computation.1 | async-start | bytes 278528
  35.0 0.7 copy-start.4
  36.7 1.6 %copy-start = (f32[3,256]{1,0:T(4,128)S(1)}, f32[3,256]{1,0:T(4,128)}, u32[]{:S(2)}) copy-start(f32[3,256]{1,0:T(4,128)} %param.8) | copy-start | bytes 9220
  37.6 0.9 copy-start.1
  37.6 1.1 %copy-start.2 = (f32[3,256]{1,0:T(4,128)S(1)}, f32[3,256]{1,0:T(4,128)}, u32[]{:S(2)}) copy-start(f32[3,256]{1,0:T(4,128)} %param.10) | copy-start | bytes 9220
  37.6 1.2 %copy-start.3 = (f32[3,256]{1,0:T(4,128)S(1)}, f32[3,256]{1,0:T(4,128)}, u32[]{:S(2)}) copy-start(f32[3,256]{1,0:T(4,128)} %param.11) | copy-start | bytes 9220
Sparse Core Ops, SparseCore 0:
  37.7 53.0 reduce-scatter.3
where the time goes:
time: 100 us; the launch traced here: 99.9 us
  waiting for transfers between devices  49.2 us (49%)
  blocking collectives  23.3 us (23%)
  between operations  14.8 us (15%)
  local copies, waits for them, and re-layouts  8.8 us (9%)
  other arithmetic  3.7 us (4%)
    unnamed x2, waiting for transfers between devices  49.2 us
    all_gather x1, blocking collectives, shards(): lax.all_gather(targets, 'stars', axis=1, tiled=True)  23.3 us
    unnamed x20, local copies, waits for them, and re-layouts  3 us
  transfers between devices with their start and end apart: 1, of which 1 were waited for; matrix products, arithmetic and copies ran while one was open for 4% of the time, Pallas kernels for 0%

commit v1 on v0

v1 whole, which is shorter than its diff:
```python
import functools

import jax
import jax.numpy as jnp
from jax import lax
from jax.experimental import pallas as pl
from jax.experimental.pallas import tpu as pltpu
from jax.sharding import PartitionSpec as P

SOFTEN = 0.0025
STEP_BASE = 0.5
LANES = 128
SUBLANES = 8
HIGHEST = lax.Precision.HIGHEST


def step_of(levels):
    return STEP_BASE * jnp.exp2(-levels.astype(jnp.float32))


def predict(pos, vel, acc, jerk, h):
    moved_pos = pos + h * (vel + h * (0.5 * acc + h * jerk * (1.0 / 6.0)))
    moved_vel = vel + h * (acc + 0.5 * h * jerk)
    return moved_pos, moved_vel


def pack_kernel(pos, vel, acc, jerk, mass, level, out):
    moved_pos, moved_vel = predict(pos[...], vel[...], acc[...], jerk[...], step_of(level[...]))
    out[0, 0:3] = moved_pos
    out[0, 3:6] = moved_vel
    out[0, 6:7] = mass[...]
    out[0, 7:8] = jnp.zeros_like(mass[...])


def add_block(stars, index, lane, target, sums):
    def row(c):
        return stars[index, pl.ds(c, 1), pl.ds(lane, LANES)]

    d = [row(c) - target[c] for c in range(3)]
    w = [row(c + 3) - target[c + 3] for c in range(3)]
    squared = (d[0] * d[0] + d[1] * d[1]) + (d[2] * d[2] + SOFTEN)
    inverse = lax.rsqrt(squared)
    inverse_sq = inverse * inverse
    weight = (row(6) * inverse) * inverse_sq
    radial = (d[0] * w[0] + d[1] * w[1] + d[2] * w[2]) * inverse_sq
    pull = [weight * c for c in d]
    return (
        tuple(s + p for s, p in zip(sums[0:3], pull))
        + tuple(s + weight * c for s, c in zip(sums[3:6], w))
        + tuple(s + radial * p for s, p in zip(sums[6:9], pull))
    )


def add_stars(stars_refs, target_ref, sums_in, sums_out):
    for tile in range(target_ref.shape[1] // SUBLANES):
        rows = pl.ds(tile * SUBLANES, SUBLANES)
        target = [target_ref[c, rows] for c in range(6)]
        if sums_in is None:
            sums = (jnp.zeros((SUBLANES, LANES), jnp.float32),) * 9
        else:
            sums = tuple(sums_in[c, rows] for c in range(9))
        for stars in stars_refs:
            pieces = stars.shape[2] // LANES

            def group(g, sums):
                for piece in range(pieces):
                    sums = add_block(stars, g, piece * LANES, target, sums)
                return sums

            sums = lax.fori_loop(0, stars.shape[0], group, sums, unroll=min(4, stars.shape[0]))
        for c in range(9):
            sums_out[c, rows] = sums[c]


def own_kernel(packed, pos, vel, acc, jerk, level, slot, target, start, sums, data, index):
    resident = packed.shape[2]
    capacity = slot.shape[1]
    data[...] = jnp.zeros_like(data)
    data[0:6] = packed[0, 0:6]
    data[8:11] = pos[...]
    data[11:14] = vel[...]
    data[14:17] = acc[...]
    data[17:20] = jerk[...]
    data[20:21] = step_of(level[...])
    index[...] = jnp.full_like(index, -1)
    index[:, 0:capacity] = slot[...]
    chosen = lax.broadcasted_iota(jnp.int32, (resident, index.shape[1]), 0) == index[...]
    picked = jnp.dot(
        data[...], chosen.astype(jnp.float32), precision=HIGHEST, preferred_element_type=jnp.float32
    )
    start[...] = picked[8:24]
    columns = picked[0:8].T
    for c in range(6):
        target[c] = jnp.broadcast_to(columns[0 : target.shape[1], c : c + 1], target.shape[1:])
    add_stars([packed], target, None, sums)


def more_kernel(stars, target, sums_in, sums_out):
    add_stars([stars], target, sums_in, sums_out)


def last_kernel(*refs):
    *stars, target, sums_in, start, count, corrected, derivatives, sums = refs
    add_stars(stars, target, sums_in, sums)
    capacity = corrected.shape[2]
    ones = jnp.ones((SUBLANES, LANES), jnp.float32)

    def total(c):
        return lax.dot_general(
            ones, sums[c], (((1,), (1,)), ((), ())), precision=HIGHEST,
            preferred_element_type=jnp.float32,
        )[0:1, 0:capacity]

    live = lax.broadcasted_iota(jnp.int32, (1, capacity), 1) < count[...]
    h = start[12:13, 0:capacity]
    for c in range(3):
        x0, v0, a0, j0 = (start[3 * k + c : 3 * k + c + 1, 0:capacity] for k in range(4))
        a1 = total(c)
        j1 = total(3 + c) - 3.0 * total(6 + c)
        v1 = v0 + 0.5 * h * (a0 + a1) + h * h * (j0 - j1) * (1.0 / 12.0)
        x1 = x0 + 0.5 * h * (v0 + v1) + h * h * (a0 - a1) * (1.0 / 12.0)
        differ = a0 - a1
        snap = 3.0 * differ + h * (j0 + 2.0 * j1)
        crackle = 2.0 * differ + h * (j0 + j1)
        for k, value in enumerate((x1, v1, a1, j1)):
            corrected[k, c : c + 1] = jnp.where(live, value, 0.0)
        for k, value in enumerate((snap, crackle)):
            derivatives[k, c : c + 1] = jnp.where(live, value, 0.0)


def shaped(*shape):
    return jax.ShapeDtypeStruct(shape, jnp.float32)


def shards(groups, position, velocity, acceleration, old_jerk, masses, levels, active_count, active_slot):
    resident = position.shape[1]
    capacity = active_slot.shape[0]
    padded = -(-capacity // LANES) * LANES
    mass = masses.reshape(1, resident)
    level = levels.reshape(1, resident)
    slot = active_slot.reshape(1, capacity)
    count = active_count.reshape(1, 1)
    state = (position, velocity, acceleration, old_jerk)

    packed = pl.pallas_call(pack_kernel, out_shape=shaped(1, 8, resident), name="pack")(*state, mass, level)

    def swap(block, mask):
        return lax.ppermute(block, "stars", [(i, i ^ mask) for i in range(groups)])

    target, start, sums = pl.pallas_call(
        own_kernel,
        out_shape=(shaped(6, capacity, LANES), shaped(16, padded), shaped(9, capacity, LANES)),
        scratch_shapes=[pltpu.VMEM((24, resident), jnp.float32), pltpu.VMEM((1, padded), jnp.int32)],
        name="own",
    )(packed, *state, level, slot)

    def more(stars, sums):
        return pl.pallas_call(
            more_kernel, out_shape=shaped(9, capacity, LANES), name="more"
        )(stars, target, sums)

    held = packed
    mask = groups // 2
    while mask > 2:
        other = swap(held, mask)
        sums = more(other, sums)
        held = jnp.concatenate([held, other], axis=0)
        mask //= 2
    rest = [swap(held, m) for m in (1, 2, 3) if m < groups]
    return pl.pallas_call(
        last_kernel,
        out_shape=(shaped(4, 3, capacity), shaped(2, 3, capacity)),
        scratch_shapes=[pltpu.VMEM((9, capacity, LANES), jnp.float32)],
        name="last",
    )(*rest, target, sums, start, count)


def solution(mesh):
    groups = mesh.shape["stars"]
    assert groups & (groups - 1) == 0
    wide = P(None, ("members", "stars"))
    flat = P(("members", "stars"))
    out = P(None, None, ("members", "stars"))
    return jax.shard_map(
        functools.partial(shards, groups),
        mesh=mesh,
        in_specs=(wide, wide, wide, wide, flat, flat, flat, flat),
        out_specs=(out, out),
        check_vma=False,
    )
```

time: 100 us -> 26.1 us (0.26)
  waiting for transfers between devices: 49.2 us -> 3.82 us
  blocking collectives: 23.3 us -> 0 us
  between operations: 14.8 us -> 1.33 us
  Pallas kernels: 0 us -> 9.05 us
  starting transfers between devices: 0.04 us -> 7.77 us
  local copies, waits for them, and re-layouts: 8.8 us -> 3.08 us
  other arithmetic: 3.7 us -> 0.71 us
    unnamed x2 -> x0, waiting for transfers between devices: 49.2 us -> none
    all_gather x1 -> x0, blocking collectives: 23.3 us -> none  [shards(): lax.all_gather(targets, 'stars', axis=1, tiled=True)]
    pallas_call x0 -> x5, Pallas kernels: none -> 9.05 us  [the longest x2 3.41 us: more(): pl.pallas_call(more_kernel, out_shape=shaped(9, capacity, LANES), name='m...]
    ppermute x0 -> x5, starting transfers between devices: none -> 7.77 us  [swap(): return lax.ppermute(block, 'stars', [(i, i ^ mask) for i in range(groups)])]
    gather x13 -> x0, local copies, waits for them, and re-layouts: 4.64 us -> none  [the longest x1 0.71 us: shards(): interval = interval_all[active_slot]]
    ppermute x0 -> x5, waiting for transfers between devices: none -> 3.82 us  [swap(): return lax.ppermute(block, 'stars', [(i, i ^ mask) for i in range(groups)])]
    pallas_call x0 -> x2, local copies, waits for them, and re-layouts: none -> 1.87 us  [shards(): pl.pallas_call(last_kernel, out_shape=(shaped(4, 3, capacity), shaped(2,...]
    unnamed x20 -> x14, local copies, waits for them, and re-layouts: 3 us -> 1.21 us
  transfers between devices with their start and end apart: 1 -> 5, of which waited for: 1 -> 2; matrix products, arithmetic and copies ran while one was open for 4% -> 0% of each run, Pallas kernels for 0% -> 20%
where the time goes in v1:
time: 26.1 us; the launch traced here: 25.8 us
  Pallas kernels  9.05 us (35%)
  starting transfers between devices  7.77 us (30%)
  waiting for transfers between devices  3.82 us (15%)
  local copies, waits for them, and re-layouts  3.08 us (12%)
  between operations  1.33 us (5%)
  other arithmetic  0.71 us (3%)
    ppermute x5, starting transfers between devices, swap(): return lax.ppermute(block, 'stars', [(i, i ^ mask) for i in range(groups)])  7.77 us
    ppermute x5, waiting for transfers between devices, swap(): return lax.ppermute(block, 'stars', [(i, i ^ mask) for i in range(groups)])  3.82 us
    pallas_call x2, Pallas kernels, more(): pl.pallas_call(more_kernel, out_shape=shaped(9, capacity, LANES), name='m...  3.41 us
    pallas_call x1, Pallas kernels, shards(): pl.pallas_call(last_kernel, out_shape=(shaped(4, 3, capacity), shaped(2,...  2.4 us
    pallas_call x2, local copies, waits for them, and re-layouts, shards(): pl.pallas_call(last_kernel, out_shape=(shaped(4, 3, capacity), shaped(2,...  1.87 us
    pallas_call x1, Pallas kernels, shards(): pl.pallas_call(own_kernel, out_shape=(shaped(6, capacity, LANES), shaped(...  1.85 us
    pallas_call x1, Pallas kernels, shards(): pl.pallas_call(pack_kernel, out_shape=shaped(1, 8, resident), name='pack')  1.39 us
    unnamed x14, local copies, waits for them, and re-layouts  1.21 us
  transfers between devices with their start and end apart: 5, of which 2 were waited for; matrix products, arithmetic and copies ran while one was open for 0% of the time, Pallas kernels for 20%

profile of v1, /device:TPU:0, one launch (start us, length us, event | category | flops | bytes accessed | tf_op | source)
XLA Modules:
  0.0 25.8 jit_solution(7839037940449730785)
XLA Ops:
  0.6 1.4 %pack.1.packed = f32[1,8,256]{2,1,0:T(8,128)} custom-call(f32[3,256]{1,0:T(4,128)} %pos.3, f32[3,256]{1,0:T(4,128)} %vel.3, f32[3,256]{1,0:T(4,128)} %acc.3, f32[3,256]{1,0:T(4,128)} %jerk.3, f32[1,256]{1,0:T(1,128)} %bitcast.7, s32[1,256]{1,0:T(1,128)} %bitcast.5), custom_call_target="tpu_custom_call" | custom-call | tf_op jit(solution)/shard_map/pack/pallas_call | solution.py:145
  2.0 0.0 copy-start
  2.0 4.1 %collective-permute-start = (f32[1,8,256]{2,1,0:T(8,128)}, f32[1,8,256]{2,1,0:T(8,128)S(1)}, u32[]{:S(2)}, u32[]{:S(2)}) collective-permute-start(f32[1,8,256]{2,1,0:T(8,128)} %pack.1.packed), channel_id=1, source_target_pairs={{0,8},{1,9},{2,10},{3,11},{4,12},{5,13},{6,14},{7,15},{8,0},{9,1},... | collective-permute-start | bytes 24584 | tf_op jit(solution)/shard_map/ppermute | solution.py:148
  6.1 1.9 %collective-permute-done.stars = f32[1,8,256]{2,1,0:T(8,128)S(1)} collective-permute-done((f32[1,8,256]{2,1,0:T(8,128)}, f32[1,8,256]{2,1,0:T(8,128)S(1)}, u32[]{:S(2)}, u32[]{:S(2)}) %collective-permute-start) | collective-permute-done | bytes 8224 | tf_op jit(solution)/shard_map/ppermute | solution.py:148
  8.0 0.0 copy-start.1
  8.0 0.7 %pad_maximum_fusion.1 = f32[2,8,256]{2,1,0:T(8,128)S(1)} fusion(f32[1,8,256]{2,1,0:T(8,128)S(1)} %collective-permute-done.stars, f32[1,8,256]{2,1,0:T(8,128)} %pack.1.packed), kind=kLoop, calls=%fused_computation.1 | loop fusion | flops 4096 | bytes 32768 | tf_op jit(solution)/shard_map/concatenate | solution.py:167
  8.7 1.8 %collective-permute-start.1 = (f32[2,8,256]{2,1,0:T(8,128)S(1)}, f32[2,8,256]{2,1,0:T(8,128)S(1)}, u32[]{:S(2)}, u32[]{:S(2)}) collective-permute-start(f32[2,8,256]{2,1,0:T(8,128)S(1)} %pad_maximum_fusion.1), channel_id=1, source_target_pairs={{0,4},{1,5},{2,6},{3,7},{4,0},{5,1},{6,2},{7,3},{8,12},{9,13},{10,... | collective-permute-start | bytes 49160 | tf_op jit(solution)/shard_map/ppermute | solution.py:148
  10.5 1.9 %collective-permute-done.1.stars = f32[2,8,256]{2,1,0:T(8,128)S(1)} collective-permute-done((f32[2,8,256]{2,1,0:T(8,128)S(1)}, f32[2,8,256]{2,1,0:T(8,128)S(1)}, u32[]{:S(2)}, u32[]{:S(2)}) %collective-permute-start.1) | collective-permute-done | bytes 16416 | tf_op jit(solution)/shard_map/ppermute | solution.py:148
  12.4 0.0 copy-done.1
  12.4 0.0 copy-done
  12.4 0.0 copy-start.2
  12.5 0.6 %copy-done.2 = f32[2,8,256]{2,1,0:T(8,128)} copy-done((f32[2,8,256]{2,1,0:T(8,128)}, f32[2,8,256]{2,1,0:T(8,128)S(1)}, u32[]{:S(2)}) %copy-start.2) | copy-done | bytes 16408
  13.0 0.0 collective-permute-start.2
  13.0 1.8 %collective-permute-start.3 = (f32[4,8,256]{2,1,0:T(8,128)S(1)}, f32[4,8,256]{2,1,0:T(8,128)S(1)}, u32[]{:S(2)}, u32[]{:S(2)}) collective-permute-start(f32[4,8,256]{2,1,0:T(8,128)S(1)} %pad_maximum_fusion), channel_id=1, source_target_pairs={{0,2},{1,3},{2,0},{3,1},{4,6},{5,7},{6,4},{7,5},{8,10},{9,11},{10,... | collective-permute-start | bytes 98312 | tf_op jit(solution)/shard_map/ppermute | solution.py:148
  14.8 0.1 collective-permute-start.4
  14.9 1.9 %own.1 = (f32[6,32,128]{2,1,0:T(8,128)}, f32[16,128]{1,0:T(8,128)}, f32[9,32,128]{2,1,0:T(8,128)}) custom-call(f32[1,8,256]{2,1,0:T(8,128)} %pack.1.packed, f32[3,256]{1,0:T(4,128)} %pos.3, f32[3,256]{1,0:T(4,128)} %vel.3, f32[3,256]{1,0:T(4,128)} %acc.3, f32[3,256]{1,0:T(4,128)} %jerk.3, s32[1,256]{1,0:T(1,128)} %bitcast.6, s32[1,32]{1,0:T(1,128)} %bitcast.8), custom_call_target="tpu_custom_call" | custom-call | tf_op jit(solution)/shard_map/own/pallas_call | solution.py:150
  17.4 1.7 %more.2.sums_in = f32[9,32,128]{2,1,0:T(8,128)} custom-call(f32[1,8,256]{2,1,0:T(8,128)} %copy-done.1, f32[6,32,128]{2,1,0:T(8,128)} %get-tuple-element.5.target.refs_3_, f32[9,32,128]{2,1,0:T(8,128)} %get-tuple-element.6.sums_in), custom_call_target="tpu_custom_call" | custom-call | tf_op jit(solution)/shard_map/more/pallas_call | solution.py:158
  19.1 1.7 %more.3.refs_4_ = f32[9,32,128]{2,1,0:T(8,128)} custom-call(f32[2,8,256]{2,1,0:T(8,128)} %copy-done.2, f32[6,32,128]{2,1,0:T(8,128)} %get-tuple-element.5.target.refs_3_, f32[9,32,128]{2,1,0:T(8,128)} %more.2.sums_in), custom_call_target="tpu_custom_call" | custom-call | tf_op jit(solution)/shard_map/more/pallas_call | solution.py:158
  20.8 0.0 collective-permute-done.2.refs_0_
  20.8 0.0 copy-start.3
  20.8 0.0 collective-permute-done.3.refs_1_
  20.8 0.0 copy-start.4
  20.8 0.0 collective-permute-done.4.refs_2_
  20.9 0.0 copy-start.5
  20.9 0.6 %copy-done.3 = f32[4,8,256]{2,1,0:T(8,128)} copy-done((f32[4,8,256]{2,1,0:T(8,128)}, f32[4,8,256]{2,1,0:T(8,128)S(1)}, u32[]{:S(2)}) %copy-start.3) | copy-done | bytes 32792
  21.4 0.0 copy-done.4
  21.5 0.0 copy-done.5
  21.5 2.4 %last.1 = (f32[4,3,32]{2,1,0:T(4,128)}, f32[2,3,32]{2,1,0:T(4,128)}) custom-call(f32[4,8,256]{2,1,0:T(8,128)} %copy-done.3, f32[4,8,256]{2,1,0:T(8,128)} %copy-done.4, f32[4,8,256]{2,1,0:T(8,128)} %copy-done.5, f32[6,32,128]{2,1,0:T(8,128)} %get-tuple-element.5.target.refs_3_, f32[9,32,128]{2,1,0:T(8,128)} %more.3.refs_4_, ...), custom_call_target="tpu_custom_call" | custom-call | tf_op jit(solution)/shard_map/last/pallas_call | solution.py:170
  23.9 0.0 copy-start.6
  23.9 1.3 %copy.10 = f32[4,3,32]{2,0,1:T(4,128)} copy(f32[4,3,32]{2,1,0:T(4,128)} %get-tuple-element.8) | data formatting | bytes 3072 | tf_op jit(solution)/shard_map/last/pallas_call | solution.py:170
  25.2 0.0 copy-done.6
  25.2 0.6 %copy.11 = f32[2,3,32]{2,0,1:T(2,128)} copy(f32[2,3,32]{2,1,0:T(4,128)S(1)} %copy-done.6) | data formatting | bytes 1536 | tf_op jit(solution)/shard_map/last/pallas_call | solution.py:170
  (1 shorter events, 0.0 us)
Async XLA Ops:
  2.0 10.4 %copy-start = (f32[1,8,256]{2,1,0:T(8,128)S(1)}, f32[1,8,256]{2,1,0:T(8,128)}, u32[]{:S(2)}) copy-start(f32[1,8,256]{2,1,0:T(8,128)} %pack.1.packed) | copy-start | bytes 24580
  2.0 6.0 %collective-permute-start = (f32[1,8,256]{2,1,0:T(8,128)}, f32[1,8,256]{2,1,0:T(8,128)S(1)}, u32[]{:S(2)}, u32[]{:S(2)}) collective-permute-start(f32[1,8,256]{2,1,0:T(8,128)} %pack.1.packed), channel_id=1, source_target_pairs={{0,8},{1,9},{2,10},{3,11},{4,12},{5,13},{6,14},{7,15},{8,0},{9,1},... | collective-permute-start | bytes 24584 | tf_op jit(solution)/shard_map/ppermute | solution.py:148
  8.0 4.4 %copy-start.1 = (f32[1,8,256]{2,1,0:T(8,128)}, f32[1,8,256]{2,1,0:T(8,128)S(1)}, u32[]{:S(2)}) copy-start(f32[1,8,256]{2,1,0:T(8,128)S(1)} %collective-permute-done.stars) | copy-start | bytes 24580
  8.7 3.7 %collective-permute-start.1 = (f32[2,8,256]{2,1,0:T(8,128)S(1)}, f32[2,8,256]{2,1,0:T(8,128)S(1)}, u32[]{:S(2)}, u32[]{:S(2)}) collective-permute-start(f32[2,8,256]{2,1,0:T(8,128)S(1)} %pad_maximum_fusion.1), channel_id=1, source_target_pairs={{0,4},{1,5},{2,6},{3,7},{4,0},{5,1},{6,2},{7,3},{8,12},{9,13},{10,... | collective-permute-start | bytes 49160 | tf_op jit(solution)/shard_map/ppermute | solution.py:148
  12.4 0.6 %copy-start.2 = (f32[2,8,256]{2,1,0:T(8,128)}, f32[2,8,256]{2,1,0:T(8,128)S(1)}, u32[]{:S(2)}) copy-start(f32[2,8,256]{2,1,0:T(8,128)S(1)} %collective-permute-done.1.stars) | copy-start | bytes 49156
  13.0 7.8 %collective-permute-start.2 = (f32[4,8,256]{2,1,0:T(8,128)S(1)}, f32[4,8,256]{2,1,0:T(8,128)S(1)}, u32[]{:S(2)}, u32[]{:S(2)}) collective-permute-start(f32[4,8,256]{2,1,0:T(8,128)S(1)} %pad_maximum_fusion), channel_id=1, source_target_pairs={{0,1},{1,0},{2,3},{3,2},{4,5},{5,4},{6,7},{7,6},{8,9},{9,8},{10,11... | collective-permute-start | bytes 98312 | tf_op jit(solution)/shard_map/ppermute | solution.py:148
  13.0 7.8 %collective-permute-start.3 = (f32[4,8,256]{2,1,0:T(8,128)S(1)}, f32[4,8,256]{2,1,0:T(8,128)S(1)}, u32[]{:S(2)}, u32[]{:S(2)}) collective-permute-start(f32[4,8,256]{2,1,0:T(8,128)S(1)} %pad_maximum_fusion), channel_id=1, source_target_pairs={{0,2},{1,3},{2,0},{3,1},{4,6},{5,7},{6,4},{7,5},{8,10},{9,11},{10,... | collective-permute-start | bytes 98312 | tf_op jit(solution)/shard_map/ppermute | solution.py:148
  14.8 6.1 %collective-permute-start.4 = (f32[4,8,256]{2,1,0:T(8,128)S(1)}, f32[4,8,256]{2,1,0:T(8,128)S(1)}, u32[]{:S(2)}, u32[]{:S(2)}) collective-permute-start(f32[4,8,256]{2,1,0:T(8,128)S(1)} %pad_maximum_fusion), channel_id=1, source_target_pairs={{0,3},{1,2},{2,1},{3,0},{4,7},{5,6},{6,5},{7,4},{8,11},{9,10},{10,... | collective-permute-start | bytes 98312 | tf_op jit(solution)/shard_map/ppermute | solution.py:148
  20.8 0.6 %copy-start.3 = (f32[4,8,256]{2,1,0:T(8,128)}, f32[4,8,256]{2,1,0:T(8,128)S(1)}, u32[]{:S(2)}) copy-start(f32[4,8,256]{2,1,0:T(8,128)S(1)} %collective-permute-done.2.refs_0_) | copy-start | bytes 98308
  20.8 0.6 %copy-start.4 = (f32[4,8,256]{2,1,0:T(8,128)}, f32[4,8,256]{2,1,0:T(8,128)S(1)}, u32[]{:S(2)}) copy-start(f32[4,8,256]{2,1,0:T(8,128)S(1)} %collective-permute-done.3.refs_1_) | copy-start | bytes 98308
  20.9 0.6 %copy-start.5 = (f32[4,8,256]{2,1,0:T(8,128)}, f32[4,8,256]{2,1,0:T(8,128)S(1)}, u32[]{:S(2)}) copy-start(f32[4,8,256]{2,1,0:T(8,128)S(1)} %collective-permute-done.4.refs_2_) | copy-start | bytes 98308
  23.9 1.3 %copy-start.6 = (f32[2,3,32]{2,1,0:T(4,128)S(1)}, f32[2,3,32]{2,1,0:T(4,128)}, u32[]{:S(2)}) copy-start(f32[2,3,32]{2,1,0:T(4,128)} %get-tuple-element.9) | copy-start | bytes 2308

commit v2 on v1

--- a/solution.py
+++ b/solution.py
@@ -24,12 +24,18 @@
     return moved_pos, moved_vel
 
 
-def pack_kernel(pos, vel, acc, jerk, mass, level, out):
-    moved_pos, moved_vel = predict(pos[...], vel[...], acc[...], jerk[...], step_of(level[...]))
+def pack_kernel(pos, vel, acc, jerk, mass, level, out, data):
+    h = step_of(level[...])
+    moved_pos, moved_vel = predict(pos[...], vel[...], acc[...], jerk[...], h)
     out[0, 0:3] = moved_pos
     out[0, 3:6] = moved_vel
     out[0, 6:7] = mass[...]
-    out[0, 7:8] = jnp.zeros_like(mass[...])
+    out[0, 7:8] = h
+    data[0:3] = pos[...]
+    data[3:6] = vel[...]
+    data[6:9] = acc[...]
+    data[9:12] = jerk[...]
+    data[12:16] = jnp.zeros_like(data[12:16])
 
 
 def add_block(stars, index, lane, target, sums):
@@ -72,24 +78,21 @@
             sums_out[c, rows] = sums[c]
 
 
-def own_kernel(packed, pos, vel, acc, jerk, level, slot, target, start, sums, data, index):
+def own_kernel(packed, data, slot, target, start, sums, index):
     resident = packed.shape[2]
     capacity = slot.shape[1]
-    data[...] = jnp.zeros_like(data)
-    data[0:6] = packed[0, 0:6]
-    data[8:11] = pos[...]
-    data[11:14] = vel[...]
-    data[14:17] = acc[...]
-    data[17:20] = jerk[...]
-    data[20:21] = step_of(level[...])
     index[...] = jnp.full_like(index, -1)
     index[:, 0:capacity] = slot[...]
     chosen = lax.broadcasted_iota(jnp.int32, (resident, index.shape[1]), 0) == index[...]
-    picked = jnp.dot(
-        data[...], chosen.astype(jnp.float32), precision=HIGHEST, preferred_element_type=jnp.float32
-    )
-    start[...] = picked[8:24]
-    columns = picked[0:8].T
+    chosen = chosen.astype(jnp.float32)
+
+    def pick(values):
+        return jnp.dot(values, chosen, precision=HIGHEST, preferred_element_type=jnp.float32)
+
+    moved = pick(packed[0])
+    start[0:16] = pick(data[...])
+    start[16:24] = moved
+    columns = moved.T
     for c in range(6):
         target[c] = jnp.broadcast_to(columns[0 : target.shape[1], c : c + 1], target.shape[1:])
     add_stars([packed], target, None, sums)
@@ -112,7 +115,7 @@
         )[0:1, 0:capacity]
 
     live = lax.broadcasted_iota(jnp.int32, (1, capacity), 1) < count[...]
-    h = start[12:13, 0:capacity]
+    h = start[23:24, 0:capacity]
     for c in range(3):
         x0, v0, a0, j0 = (start[3 * k + c : 3 * k + c + 1, 0:capacity] for k in range(4))
         a1 = total(c)
@@ -123,13 +126,18 @@
         snap = 3.0 * differ + h * (j0 + 2.0 * j1)
         crackle = 2.0 * differ + h * (j0 + j1)
         for k, value in enumerate((x1, v1, a1, j1)):
-            corrected[k, c : c + 1] = jnp.where(live, value, 0.0)
+            corrected[c, k : k + 1] = jnp.where(live, value, 0.0)
         for k, value in enumerate((snap, crackle)):
-            derivatives[k, c : c + 1] = jnp.where(live, value, 0.0)
+            derivatives[c, k : k + 1] = jnp.where(live, value, 0.0)
 
 
-def shaped(*shape):
-    return jax.ShapeDtypeStruct(shape, jnp.float32)
+def call(kernel, outs, *args, inside=True, **kwargs):
+    space = pltpu.VMEM if inside else jax.ShapeDtypeStruct
+    return pl.pallas_call(kernel, out_shape=tuple(space(o, jnp.float32) for o in outs), **kwargs)(*args)
+
+
+def keep(x):
+    return pltpu.with_memory_space_constraint(x, pltpu.VMEM)
 
 
 def shards(groups, position, velocity, acceleration, old_jerk, masses, levels, active_count, active_slot):
@@ -140,39 +148,33 @@
     level = levels.reshape(1, resident)
     slot = active_slot.reshape(1, capacity)
     count = active_count.reshape(1, 1)
-    state = (position, velocity, acceleration, old_jerk)
-
-    packed = pl.pallas_call(pack_kernel, out_shape=shaped(1, 8, resident), name="pack")(*state, mass, level)
+    packed, data = call(
+        pack_kernel, ((1, 8, resident), (16, resident)),
+        position, velocity, acceleration, old_jerk, mass, level, name="pack",
+    )
 
     def swap(block, mask):
         return lax.ppermute(block, "stars", [(i, i ^ mask) for i in range(groups)])
 
-    target, start, sums = pl.pallas_call(
-        own_kernel,
-        out_shape=(shaped(6, capacity, LANES), shaped(16, padded), shaped(9, capacity, LANES)),
-        scratch_shapes=[pltpu.VMEM((24, resident), jnp.float32), pltpu.VMEM((1, padded), jnp.int32)],
-        name="own",
-    )(packed, *state, level, slot)
-
-    def more(stars, sums):
-        return pl.pallas_call(
-            more_kernel, out_shape=shaped(9, capacity, LANES), name="more"
-        )(stars, target, sums)
-
+    all_sums = (9, capacity, LANES)
+    target, start, sums = call(
+        own_kernel, ((6, capacity, LANES), (24, padded), all_sums), keep(packed), keep(data), slot,
+        scratch_shapes=[pltpu.VMEM((1, padded), jnp.int32)], name="own",
+    )
     held = packed
     mask = groups // 2
     while mask > 2:
         other = swap(held, mask)
-        sums = more(other, sums)
+        (sums,) = call(more_kernel, (all_sums,), keep(other), keep(target), keep(sums), name="more")
         held = jnp.concatenate([held, other], axis=0)
         mask //= 2
     rest = [swap(held, m) for m in (1, 2, 3) if m < groups]
-    return pl.pallas_call(
-        last_kernel,
-        out_shape=(shaped(4, 3, capacity), shaped(2, 3, capacity)),
-        scratch_shapes=[pltpu.VMEM((9, capacity, LANES), jnp.float32)],
-        name="last",
-    )(*rest, target, sums, start, count)
+    corrected, derivatives = call(
+        last_kernel, ((3, 4, capacity), (3, 2, capacity)),
+        *(keep(x) for x in (*rest, target, sums, start)), count, inside=False,
+        scratch_shapes=[pltpu.VMEM(all_sums, jnp.float32)], name="last",
+    )
+    return jnp.swapaxes(corrected, 0, 1), jnp.swapaxes(derivatives, 0, 1)
 
 
 def solution(mesh):

time: 26.1 us -> 17.7 us (0.68)
  Pallas kernels: 9.05 us -> 3.38 us
  local copies, waits for them, and re-layouts: 3.08 us -> 0.01 us
  waiting for transfers between devices: 3.82 us -> 4.81 us
  other arithmetic: 0.71 us -> 0.01 us
    pallas_call x5, Pallas kernels: 9.05 us -> 3.38 us  [call(): pl.pallas_call(kernel, out_shape=tuple((space(o, jnp.float32) for o in ou...]
    pallas_call x2 -> x0, local copies, waits for them, and re-layouts: 1.87 us -> none  [shards(): pl.pallas_call(last_kernel, out_shape=(shaped(4, 3, capacity), shaped(2,...]
    unnamed x14 -> x2, local copies, waits for them, and re-layouts: 1.21 us -> 0.01 us
    ppermute x5, waiting for transfers between devices: 3.82 us -> 4.81 us  [swap(): return lax.ppermute(block, 'stars', [(i, i ^ mask) for i in range(groups)])]
    concatenate x2 -> x1, other arithmetic: 0.71 us -> 0.01 us  [shards(): held = jnp.concatenate([held, other], axis=0)]
  transfers between devices with their start and end apart: 5 -> 5, of which waited for: 2 -> 4; matrix products, arithmetic and copies ran while one was open for 0% -> 0% of each run, Pallas kernels for 20% -> 7%
where the time goes in v2:
time: 17.7 us; the launch traced here: 17.5 us
  starting transfers between devices  7.97 us (45%)
  waiting for transfers between devices  4.81 us (27%)
  Pallas kernels  3.38 us (19%)
  between operations  1.32 us (7%)
    ppermute x5, starting transfers between devices, swap(): return lax.ppermute(block, 'stars', [(i, i ^ mask) for i in range(groups)])  7.97 us
    ppermute x5, waiting for transfers between devices, swap(): return lax.ppermute(block, 'stars', [(i, i ^ mask) for i in range(groups)])  4.81 us
    pallas_call x5, Pallas kernels, call(): pl.pallas_call(kernel, out_shape=tuple((space(o, jnp.float32) for o in ou...  3.38 us
  transfers between devices with their start and end apart: 5, of which 4 were waited for; matrix products, arithmetic and copies ran while one was open for 0% of the time, Pallas kernels for 7%

profile of v2, /device:TPU:0, one launch (start us, length us, event | category | flops | bytes accessed | tf_op | source)
XLA Modules:
  0.0 17.5 jit_solution(15696186226995343481)
XLA Ops:
  0.6 0.8 %pack.1 = (f32[1,8,256]{2,1,0:T(8,128)S(1)}, f32[16,256]{1,0:T(8,128)S(1)}) custom-call(f32[3,256]{1,0:T(4,128)} %pos.1, f32[3,256]{1,0:T(4,128)} %vel.1, f32[3,256]{1,0:T(4,128)} %acc.1, f32[3,256]{1,0:T(4,128)} %jerk.1, f32[1,256]{1,0:T(1,128)} %bitcast.7, s32[1,256]{1,0:T(1,128)} %bitcast.8), custom_call_target="tpu_custom_call" | custom-call | tf_op jit(solution)/shard_map/pack/pallas_call | solution.py:136
  1.4 4.1 %collective-permute-start = (f32[1,8,256]{2,1,0:T(8,128)S(1)}, f32[1,8,256]{2,1,0:T(8,128)S(1)}, u32[]{:S(2)}, u32[]{:S(2)}) collective-permute-start(f32[1,8,256]{2,1,0:T(8,128)S(1)} %get-tuple-element.9.packed), channel_id=1, source_target_pairs={{0,8},{1,9},{2,10},{3,11},{4,12},{5,13},{6,14},{7,15},{8,0},{9,1},... | collective-permute-start | bytes 24584 | tf_op jit(solution)/shard_map/ppermute | solution.py:157
  5.5 1.6 %collective-permute-done.stars = f32[1,8,256]{2,1,0:T(8,128)S(1)} collective-permute-done((f32[1,8,256]{2,1,0:T(8,128)S(1)}, f32[1,8,256]{2,1,0:T(8,128)S(1)}, u32[]{:S(2)}, u32[]{:S(2)}) %collective-permute-start) | collective-permute-done | bytes 8224 | tf_op jit(solution)/shard_map/ppermute | solution.py:157
  7.2 1.9 %collective-permute-start.1 = (f32[2,8,256]{2,1,0:T(8,128)S(1)}, f32[2,8,256]{2,1,0:T(8,128)S(1)}, u32[]{:S(2)}, u32[]{:S(2)}) collective-permute-start(f32[2,8,256]{2,1,0:T(8,128)S(1)} %pad_maximum_fusion), channel_id=1, source_target_pairs={{0,4},{1,5},{2,6},{3,7},{4,0},{5,1},{6,2},{7,3},{8,12},{9,13},{10,... | collective-permute-start | bytes 49160 | tf_op jit(solution)/shard_map/ppermute | solution.py:157
  9.1 1.8 %collective-permute-done.1.stars = f32[2,8,256]{2,1,0:T(8,128)S(1)} collective-permute-done((f32[2,8,256]{2,1,0:T(8,128)S(1)}, f32[2,8,256]{2,1,0:T(8,128)S(1)}, u32[]{:S(2)}, u32[]{:S(2)}) %collective-permute-start.1) | collective-permute-done | bytes 16416 | tf_op jit(solution)/shard_map/ppermute | solution.py:157
  10.9 0.0 collective-permute-start.2
  10.9 1.8 %collective-permute-start.3 = (f32[4,8,256]{2,1,0:T(8,128)S(1)}, f32[4,8,256]{2,1,0:T(8,128)S(1)}, u32[]{:S(2)}, u32[]{:S(2)}) collective-permute-start(f32[4,8,256]{2,1,0:T(8,128)S(1)} %constant_dynamic-update-slice_fusion), channel_id=1, source_target_pairs={{0,2},{1,3},{2,0},{3,1},{4,6},{5,7},{6,4},{7,5},{8,10},{9,11},{10,... | collective-permute-start | bytes 98312 | tf_op jit(solution)/shard_map/ppermute | solution.py:157
  12.7 0.1 collective-permute-start.4
  13.5 1.0 %own.1 = (f32[6,32,128]{2,1,0:T(8,128)S(1)}, f32[24,128]{1,0:T(8,128)S(1)}, f32[9,32,128]{2,1,0:T(8,128)S(1)}) custom-call(f32[1,8,256]{2,1,0:T(8,128)S(1)} %get-tuple-element.9.packed, f32[16,256]{1,0:T(8,128)S(1)} %get-tuple-element.10.data, s32[1,32]{1,0:T(1,128)} %bitcast.9), custom_call_target="tpu_custom_call" | custom-call | tf_op jit(solution)/shard_map/own/pallas_call | solution.py:136
  14.6 0.1 more.2.sums_in
  14.6 0.1 more.3.refs_4_
  14.7 0.0 collective-permute-done.2.refs_0_
  14.7 0.1 collective-permute-done.3.refs_1_
  14.8 1.2 %collective-permute-done.4.refs_2_ = f32[4,8,256]{2,1,0:T(8,128)S(1)} collective-permute-done((f32[4,8,256]{2,1,0:T(8,128)S(1)}, f32[4,8,256]{2,1,0:T(8,128)S(1)}, u32[]{:S(2)}, u32[]{:S(2)}) %collective-permute-start.4) | collective-permute-done | bytes 32800 | tf_op jit(solution)/shard_map/ppermute | solution.py:157
  16.1 1.4 %last.1 = (f32[3,4,32]{2,1,0:T(4,128)}, f32[3,2,32]{2,1,0:T(2,128)}) custom-call(f32[4,8,256]{2,1,0:T(8,128)S(1)} %collective-permute-done.2.refs_0_, f32[4,8,256]{2,1,0:T(8,128)S(1)} %collective-permute-done.3.refs_1_, f32[4,8,256]{2,1,0:T(8,128)S(1)} %collective-permute-done.4.refs_2_, f32[6,32,128]{2,1,0:T(8,128)S(1)} %get-tuple-element.11.target.refs_3_, ...), custom_call_target="tpu_custom_call" | custom-call | tf_op jit(solution)/shard_map/last/pallas_call | solution.py:136
  (4 shorter events, 0.0 us)
Async XLA Ops:
  1.4 5.8 %collective-permute-start = (f32[1,8,256]{2,1,0:T(8,128)S(1)}, f32[1,8,256]{2,1,0:T(8,128)S(1)}, u32[]{:S(2)}, u32[]{:S(2)}) collective-permute-start(f32[1,8,256]{2,1,0:T(8,128)S(1)} %get-tuple-element.9.packed), channel_id=1, source_target_pairs={{0,8},{1,9},{2,10},{3,11},{4,12},{5,13},{6,14},{7,15},{8,0},{9,1},... | collective-permute-start | bytes 24584 | tf_op jit(solution)/shard_map/ppermute | solution.py:157
  7.2 3.7 %collective-permute-start.1 = (f32[2,8,256]{2,1,0:T(8,128)S(1)}, f32[2,8,256]{2,1,0:T(8,128)S(1)}, u32[]{:S(2)}, u32[]{:S(2)}) collective-permute-start(f32[2,8,256]{2,1,0:T(8,128)S(1)} %pad_maximum_fusion), channel_id=1, source_target_pairs={{0,4},{1,5},{2,6},{3,7},{4,0},{5,1},{6,2},{7,3},{8,12},{9,13},{10,... | collective-permute-start | bytes 49160 | tf_op jit(solution)/shard_map/ppermute | solution.py:157
  10.9 3.8 %collective-permute-start.2 = (f32[4,8,256]{2,1,0:T(8,128)S(1)}, f32[4,8,256]{2,1,0:T(8,128)S(1)}, u32[]{:S(2)}, u32[]{:S(2)}) collective-permute-start(f32[4,8,256]{2,1,0:T(8,128)S(1)} %constant_dynamic-update-slice_fusion), channel_id=1, source_target_pairs={{0,1},{1,0},{2,3},{3,2},{4,5},{5,4},{6,7},{7,6},{8,9},{9,8},{10,11... | collective-permute-start | bytes 98312 | tf_op jit(solution)/shard_map/ppermute | solution.py:157
  10.9 3.9 %collective-permute-start.3 = (f32[4,8,256]{2,1,0:T(8,128)S(1)}, f32[4,8,256]{2,1,0:T(8,128)S(1)}, u32[]{:S(2)}, u32[]{:S(2)}) collective-permute-start(f32[4,8,256]{2,1,0:T(8,128)S(1)} %constant_dynamic-update-slice_fusion), channel_id=1, source_target_pairs={{0,2},{1,3},{2,0},{3,1},{4,6},{5,7},{6,4},{7,5},{8,10},{9,11},{10,... | collective-permute-start | bytes 98312 | tf_op jit(solution)/shard_map/ppermute | solution.py:157
  12.7 3.3 %collective-permute-start.4 = (f32[4,8,256]{2,1,0:T(8,128)S(1)}, f32[4,8,256]{2,1,0:T(8,128)S(1)}, u32[]{:S(2)}, u32[]{:S(2)}) collective-permute-start(f32[4,8,256]{2,1,0:T(8,128)S(1)} %constant_dynamic-update-slice_fusion), channel_id=1, source_target_pairs={{0,3},{1,2},{2,1},{3,0},{4,7},{5,6},{6,5},{7,4},{8,11},{9,10},{10,... | collective-permute-start | bytes 98312 | tf_op jit(solution)/shard_map/ppermute | solution.py:157

commit v3 on v2

--- a/solution.py
+++ b/solution.py
@@ -24,18 +24,21 @@
     return moved_pos, moved_vel
 
 
-def pack_kernel(pos, vel, acc, jerk, mass, level, out, data):
-    h = step_of(level[...])
+def pack_kernel(pos, vel, acc, jerk, mass, level, slot, out, data):
+    resident = pos.shape[1]
+    capacity = slot.shape[0]
+    h = step_of(level[...]).reshape(1, resident)
     moved_pos, moved_vel = predict(pos[...], vel[...], acc[...], jerk[...], h)
     out[0, 0:3] = moved_pos
     out[0, 3:6] = moved_vel
-    out[0, 6:7] = mass[...]
+    out[0, 6:7] = mass[...].reshape(1, resident)
     out[0, 7:8] = h
     data[0:3] = pos[...]
     data[3:6] = vel[...]
     data[6:9] = acc[...]
     data[9:12] = jerk[...]
-    data[12:16] = jnp.zeros_like(data[12:16])
+    data[12:16] = jnp.full((4, resident), -1.0, jnp.float32)
+    data[12:13, 0:capacity] = slot[...].astype(jnp.float32).reshape(1, capacity)
 
 
 def add_block(stars, index, lane, target, sums):
@@ -78,13 +81,12 @@
             sums_out[c, rows] = sums[c]
 
 
-def own_kernel(packed, data, slot, target, start, sums, index):
+def own_kernel(packed, data, target, start, sums):
     resident = packed.shape[2]
-    capacity = slot.shape[1]
-    index[...] = jnp.full_like(index, -1)
-    index[:, 0:capacity] = slot[...]
-    chosen = lax.broadcasted_iota(jnp.int32, (resident, index.shape[1]), 0) == index[...]
-    chosen = chosen.astype(jnp.float32)
+    padded = start.shape[1]
+    slot = data[12:13, 0:padded].astype(jnp.int32)
+    chosen = lax.broadcasted_iota(jnp.int32, (resident, padded), 0) == slot
+    chosen = jnp.where(chosen, 1.0, 0.0)
 
     def pick(values):
         return jnp.dot(values, chosen, precision=HIGHEST, preferred_element_type=jnp.float32)
@@ -103,7 +105,7 @@
 
 
 def last_kernel(*refs):
-    *stars, target, sums_in, start, count, corrected, derivatives, sums = refs
+    *stars, target, sums_in, start, live_ref, corrected, derivatives, sums = refs
     add_stars(stars, target, sums_in, sums)
     capacity = corrected.shape[2]
     ones = jnp.ones((SUBLANES, LANES), jnp.float32)
@@ -114,7 +116,7 @@
             preferred_element_type=jnp.float32,
         )[0:1, 0:capacity]
 
-    live = lax.broadcasted_iota(jnp.int32, (1, capacity), 1) < count[...]
+    live = live_ref[...] > 0.0
     h = start[23:24, 0:capacity]
     for c in range(3):
         x0, v0, a0, j0 = (start[3 * k + c : 3 * k + c + 1, 0:capacity] for k in range(4))
@@ -144,34 +146,43 @@
     resident = position.shape[1]
     capacity = active_slot.shape[0]
     padded = -(-capacity // LANES) * LANES
-    mass = masses.reshape(1, resident)
-    level = levels.reshape(1, resident)
-    slot = active_slot.reshape(1, capacity)
-    count = active_count.reshape(1, 1)
+    assert padded <= resident
     packed, data = call(
         pack_kernel, ((1, 8, resident), (16, resident)),
-        position, velocity, acceleration, old_jerk, mass, level, name="pack",
+        position, velocity, acceleration, old_jerk, masses, levels, active_slot, name="pack",
     )
 
     def swap(block, mask):
         return lax.ppermute(block, "stars", [(i, i ^ mask) for i in range(groups)])
 
     all_sums = (9, capacity, LANES)
+
+    def more(stars, sums):
+        return call(more_kernel, (all_sums,), keep(stars), keep(target), keep(sums), name="more")[0]
+
     target, start, sums = call(
-        own_kernel, ((6, capacity, LANES), (24, padded), all_sums), keep(packed), keep(data), slot,
-        scratch_shapes=[pltpu.VMEM((1, padded), jnp.int32)], name="own",
-    )
+        own_kernel, ((6, capacity, LANES), (24, padded), all_sums), keep(packed), keep(data), name="own",
+    )
+    slots = lax.broadcasted_iota(jnp.int32, (1, capacity), 1)
+    live = active_count
     held = packed
     mask = groups // 2
-    while mask > 2:
-        other = swap(held, mask)
-        (sums,) = call(more_kernel, (all_sums,), keep(other), keep(target), keep(sums), name="more")
+    while mask > 1:
+        other = swap(held, mask | 1)
+        if mask == 2:
+            early = swap(held, 1)
+        other, sums, live = lax.optimization_barrier((other, sums, live))
+        if mask == groups // 2:
+            live = jnp.where(slots < live, 1.0, 0.0)
+        if mask == 2:
+            late = swap(other, 1)
+            sums = more(early, sums)
+        sums = more(other, sums)
         held = jnp.concatenate([held, other], axis=0)
         mask //= 2
-    rest = [swap(held, m) for m in (1, 2, 3) if m < groups]
     corrected, derivatives = call(
         last_kernel, ((3, 4, capacity), (3, 2, capacity)),
-        *(keep(x) for x in (*rest, target, sums, start)), count, inside=False,
+        *(keep(x) for x in (late, target, sums, start, live)), inside=False,
         scratch_shapes=[pltpu.VMEM(all_sums, jnp.float32)], name="last",
     )
     return jnp.swapaxes(corrected, 0, 1), jnp.swapaxes(derivatives, 0, 1)

time: 17.7 us -> 15.6 us (0.88)
  waiting for transfers between devices: 4.81 us -> 3.39 us
  Pallas kernels: 3.38 us -> 2.75 us
    ppermute x5, waiting for transfers between devices: 4.81 us -> 3.39 us  [swap(): return lax.ppermute(block, 'stars', [(i, i ^ mask) for i in range(groups)])]
    pallas_call x5 -> x7, Pallas kernels: 3.38 us -> 2.75 us  [call(): pl.pallas_call(kernel, out_shape=tuple((space(o, jnp.float32) for o in ou...]
  transfers between devices with their start and end apart: 5 -> 5, of which waited for: 4 -> 4; matrix products, arithmetic and copies ran while one was open for 0% -> 0% of each run, Pallas kernels for 7% -> 6%
where the time goes in v3:
time: 15.6 us; the launch traced here: 15.4 us
  starting transfers between devices  7.96 us (51%)
  waiting for transfers between devices  3.39 us (22%)
  Pallas kernels  2.75 us (18%)
  between operations  1.32 us (8%)
    ppermute x5, starting transfers between devices, swap(): return lax.ppermute(block, 'stars', [(i, i ^ mask) for i in range(groups)])  7.96 us
    ppermute x5, waiting for transfers between devices, swap(): return lax.ppermute(block, 'stars', [(i, i ^ mask) for i in range(groups)])  3.39 us
    pallas_call x7, Pallas kernels, call(): pl.pallas_call(kernel, out_shape=tuple((space(o, jnp.float32) for o in ou...  2.75 us
  transfers between devices with their start and end apart: 5, of which 4 were waited for; matrix products, arithmetic and copies ran while one was open for 0% of the time, Pallas kernels for 6%

profile of v3, /device:TPU:0, one launch (start us, length us, event | category | flops | bytes accessed | tf_op | source)
XLA Modules:
  0.0 15.4 jit_solution(6698459716458175509)
XLA Ops:
  0.6 0.8 %pack.1 = (f32[1,8,256]{2,1,0:T(8,128)S(1)}, f32[16,256]{1,0:T(8,128)S(1)}) custom-call(f32[3,256]{1,0:T(4,128)} %pos.1, f32[3,256]{1,0:T(4,128)} %vel.1, f32[3,256]{1,0:T(4,128)} %acc.1, f32[3,256]{1,0:T(4,128)} %jerk.1, f32[256]{0:T(256)} %mass.1, s32[256]{0:T(256)} %level.1, s32[32]{0:T(128)} %slot.1), custom_call_target="tpu_custom_call" | custom-call | tf_op jit(solution)/shard_map/pack/pallas_call | solution.py:138
  1.4 3.6 %collective-permute-start = (f32[1,8,256]{2,1,0:T(8,128)S(1)}, f32[1,8,256]{2,1,0:T(8,128)S(1)}, u32[]{:S(2)}, u32[]{:S(2)}) collective-permute-start(f32[1,8,256]{2,1,0:T(8,128)S(1)} %get-tuple-element.18.packed), channel_id=1, source_target_pairs={{0,9},{1,8},{2,11},{3,10},{4,13},{5,12},{6,15},{7,14},{8,1},{9,0},... | collective-permute-start | bytes 24584 | tf_op jit(solution)/shard_map/ppermute | solution.py:156
  5.7 0.4 %own.1 = (f32[6,32,128]{2,1,0:T(8,128)S(1)}, f32[24,128]{1,0:T(8,128)S(1)}, f32[9,32,128]{2,1,0:T(8,128)S(1)}) custom-call(f32[1,8,256]{2,1,0:T(8,128)S(1)} %get-tuple-element.18.packed, f32[16,256]{1,0:T(8,128)S(1)} %get-tuple-element.19.data), custom_call_target="tpu_custom_call" | custom-call | tf_op jit(solution)/shard_map/own/pallas_call | solution.py:138
  6.0 0.3 %collective-permute-done.stars = f32[1,8,256]{2,1,0:T(8,128)S(1)} collective-permute-done((f32[1,8,256]{2,1,0:T(8,128)S(1)}, f32[1,8,256]{2,1,0:T(8,128)S(1)}, u32[]{:S(2)}, u32[]{:S(2)}) %collective-permute-start) | collective-permute-done | bytes 8224 | tf_op jit(solution)/shard_map/ppermute | solution.py:156
  6.4 1.9 %collective-permute-start.1 = (f32[2,8,256]{2,1,0:T(8,128)S(1)}, f32[2,8,256]{2,1,0:T(8,128)S(1)}, u32[]{:S(2)}, u32[]{:S(2)}) collective-permute-start(f32[2,8,256]{2,1,0:T(8,128)S(1)} %pad_maximum_fusion), channel_id=1, source_target_pairs={{0,5},{1,4},{2,7},{3,6},{4,1},{5,0},{6,3},{7,2},{8,13},{9,12},{10,... | collective-permute-start | bytes 49160 | tf_op jit(solution)/shard_map/ppermute | solution.py:156
  8.2 0.1 more.4.sums_in
  8.3 1.4 %collective-permute-done.1.stars = f32[2,8,256]{2,1,0:T(8,128)S(1)} collective-permute-done((f32[2,8,256]{2,1,0:T(8,128)S(1)}, f32[2,8,256]{2,1,0:T(8,128)S(1)}, u32[]{:S(2)}, u32[]{:S(2)}) %collective-permute-start.1) | collective-permute-done | bytes 16416 | tf_op jit(solution)/shard_map/ppermute | solution.py:156
  9.7 1.6 %collective-permute-start.2 = (f32[4,8,256]{2,1,0:T(8,128)S(1)}, f32[4,8,256]{2,1,0:T(8,128)S(1)}, u32[]{:S(2)}, u32[]{:S(2)}) collective-permute-start(f32[4,8,256]{2,1,0:T(8,128)S(1)} %constant_dynamic-update-slice_fusion), channel_id=1, source_target_pairs={{0,3},{1,2},{2,1},{3,0},{4,7},{5,6},{6,5},{7,4},{8,11},{9,10},{10,... | collective-permute-start | bytes 98312 | tf_op jit(solution)/shard_map/ppermute | solution.py:156
  11.3 0.4 %collective-permute-start.4 = (f32[4,8,256]{2,1,0:T(8,128)S(1)}, f32[4,8,256]{2,1,0:T(8,128)S(1)}, u32[]{:S(2)}, u32[]{:S(2)}) collective-permute-start(f32[4,8,256]{2,1,0:T(8,128)S(1)} %constant_dynamic-update-slice_fusion), channel_id=1, source_target_pairs={{0,1},{1,0},{2,3},{3,2},{4,5},{5,4},{6,7},{7,6},{8,9},{9,8},{10,11... | collective-permute-start | bytes 98312 | tf_op jit(solution)/shard_map/ppermute | solution.py:156
  11.7 0.1 more.5.sums_in
  11.8 1.2 %collective-permute-done.2.stars = f32[4,8,256]{2,1,0:T(8,128)S(1)} collective-permute-done((f32[4,8,256]{2,1,0:T(8,128)S(1)}, f32[4,8,256]{2,1,0:T(8,128)S(1)}, u32[]{:S(2)}, u32[]{:S(2)}) %collective-permute-start.2) | collective-permute-done | bytes 32800 | tf_op jit(solution)/shard_map/ppermute | solution.py:156
  13.0 0.5 %collective-permute-start.3 = (f32[4,8,256]{2,1,0:T(8,128)S(1)}, f32[4,8,256]{2,1,0:T(8,128)S(1)}, u32[]{:S(2)}, u32[]{:S(2)}) collective-permute-start(f32[4,8,256]{2,1,0:T(8,128)S(1)} %collective-permute-done.2.stars), channel_id=1, source_target_pairs={{0,1},{1,0},{2,3},{3,2},{4,5},{5,4},{6,7},{7,6},{8,9},{9,8},{10,11... | collective-permute-start | bytes 98312 | tf_op jit(solution)/shard_map/ppermute | solution.py:156
  13.5 0.0 collective-permute-done.4.stars
  13.5 0.2 %more.6.sums_in = f32[9,32,128]{2,1,0:T(8,128)S(1)} custom-call(f32[4,8,256]{2,1,0:T(8,128)S(1)} %collective-permute-done.4.stars, f32[6,32,128]{2,1,0:T(8,128)S(1)} %get-tuple-element.22.target.refs_1_, f32[9,32,128]{2,1,0:T(8,128)S(1)} %more.5.sums_in), custom_call_target="tpu_custom_call" | custom-call | tf_op jit(solution)/shard_map/more/pallas_call | solution.py:138
  13.7 0.2 %more.7.refs_2_ = f32[9,32,128]{2,1,0:T(8,128)S(1)} custom-call(f32[4,8,256]{2,1,0:T(8,128)S(1)} %collective-permute-done.2.stars, f32[6,32,128]{2,1,0:T(8,128)S(1)} %get-tuple-element.22.target.refs_1_, f32[9,32,128]{2,1,0:T(8,128)S(1)} %more.6.sums_in), custom_call_target="tpu_custom_call" | custom-call | tf_op jit(solution)/shard_map/more/pallas_call | solution.py:138
  13.9 0.5 %collective-permute-done.3.refs_0_ = f32[4,8,256]{2,1,0:T(8,128)S(1)} collective-permute-done((f32[4,8,256]{2,1,0:T(8,128)S(1)}, f32[4,8,256]{2,1,0:T(8,128)S(1)}, u32[]{:S(2)}, u32[]{:S(2)}) %collective-permute-start.3) | collective-permute-done | bytes 32800 | tf_op jit(solution)/shard_map/ppermute | solution.py:156
  14.4 1.1 %last.1 = (f32[3,4,32]{2,1,0:T(4,128)}, f32[3,2,32]{2,1,0:T(2,128)}) custom-call(f32[4,8,256]{2,1,0:T(8,128)S(1)} %collective-permute-done.3.refs_0_, f32[6,32,128]{2,1,0:T(8,128)S(1)} %get-tuple-element.22.target.refs_1_, f32[9,32,128]{2,1,0:T(8,128)S(1)} %more.7.refs_2_, f32[24,128]{1,0:T(8,128)S(1)} %get-tuple-element.30.refs_3_, ...), custom_call_target="tpu_custom_call" | custom-call | tf_op jit(solution)/shard_map/last/pallas_call | solution.py:138
  (5 shorter events, 0.0 us)
Async XLA Ops:
  1.4 4.9 %collective-permute-start = (f32[1,8,256]{2,1,0:T(8,128)S(1)}, f32[1,8,256]{2,1,0:T(8,128)S(1)}, u32[]{:S(2)}, u32[]{:S(2)}) collective-permute-start(f32[1,8,256]{2,1,0:T(8,128)S(1)} %get-tuple-element.18.packed), channel_id=1, source_target_pairs={{0,9},{1,8},{2,11},{3,10},{4,13},{5,12},{6,15},{7,14},{8,1},{9,0},... | collective-permute-start | bytes 24584 | tf_op jit(solution)/shard_map/ppermute | solution.py:156
  6.4 3.3 %collective-permute-start.1 = (f32[2,8,256]{2,1,0:T(8,128)S(1)}, f32[2,8,256]{2,1,0:T(8,128)S(1)}, u32[]{:S(2)}, u32[]{:S(2)}) collective-permute-start(f32[2,8,256]{2,1,0:T(8,128)S(1)} %pad_maximum_fusion), channel_id=1, source_target_pairs={{0,5},{1,4},{2,7},{3,6},{4,1},{5,0},{6,3},{7,2},{8,13},{9,12},{10,... | collective-permute-start | bytes 49160 | tf_op jit(solution)/shard_map/ppermute | solution.py:156
  9.7 3.3 %collective-permute-start.2 = (f32[4,8,256]{2,1,0:T(8,128)S(1)}, f32[4,8,256]{2,1,0:T(8,128)S(1)}, u32[]{:S(2)}, u32[]{:S(2)}) collective-permute-start(f32[4,8,256]{2,1,0:T(8,128)S(1)} %constant_dynamic-update-slice_fusion), channel_id=1, source_target_pairs={{0,3},{1,2},{2,1},{3,0},{4,7},{5,6},{6,5},{7,4},{8,11},{9,10},{10,... | collective-permute-start | bytes 98312 | tf_op jit(solution)/shard_map/ppermute | solution.py:156
  11.3 2.2 %collective-permute-start.4 = (f32[4,8,256]{2,1,0:T(8,128)S(1)}, f32[4,8,256]{2,1,0:T(8,128)S(1)}, u32[]{:S(2)}, u32[]{:S(2)}) collective-permute-start(f32[4,8,256]{2,1,0:T(8,128)S(1)} %constant_dynamic-update-slice_fusion), channel_id=1, source_target_pairs={{0,1},{1,0},{2,3},{3,2},{4,5},{5,4},{6,7},{7,6},{8,9},{9,8},{10,11... | collective-permute-start | bytes 98312 | tf_op jit(solution)/shard_map/ppermute | solution.py:156
  13.0 1.3 %collective-permute-start.3 = (f32[4,8,256]{2,1,0:T(8,128)S(1)}, f32[4,8,256]{2,1,0:T(8,128)S(1)}, u32[]{:S(2)}, u32[]{:S(2)}) collective-permute-start(f32[4,8,256]{2,1,0:T(8,128)S(1)} %collective-permute-done.2.stars), channel_id=1, source_target_pairs={{0,1},{1,0},{2,3},{3,2},{4,5},{5,4},{6,7},{7,6},{8,9},{9,8},{10,11... | collective-permute-start | bytes 98312 | tf_op jit(solution)/shard_map/ppermute | solution.py:156
